TPU v7x, 32 devices: a whole 2x2x4 slice. The times are simulated.
32 devices in a mesh: grp: 8 (over y, x, core), rep: 4 (over z).
Axes of the slice: x: 2, y: 2, z: 4, core: 2. Of those that a mesh axis runs over, the one named last changes fastest.
Arguments:
- momentum: bfloat16 [256, 4096], P(('grp', 'rep')), may hold values from -6 to 6
- picked: int32 [256, 32], P(('grp', 'rep')), may hold values from 0 to 4095, as said below
- owner_span_order: int32 [8], replicated, may hold values from 0 to 7, each once
Outputs:
- update: bfloat16 [8, 4096], replicated
- residual_momentum: bfloat16 [256, 4096], P(('grp', 'rep'))
Inputs may be any that keep to these rules, and one draw needn't show every extreme that they name: `picked`: the 32 numbers of a row are different. `owner_span_order`: each span stands once.
All inputs are finite; a program needn't handle non-finite values.
Results may differ from a plain program's by a relative error of at most 0.013.
Values may be sent and summed in bfloat16 or wider, within the bound.
A program may use at most 64 MiB of HBM per device.

v0:
```python
import math
import jax
import jax.numpy as jnp
from jax import lax
from jax.sharding import PartitionSpec as P

BLOCK = 64
TOPK = 32
CH_OWN = 1


def dct_cosines(points):
    freq = jnp.arange(points, dtype=jnp.float32)[:, None]
    place = jnp.arange(points, dtype=jnp.float32)[None, :]
    values = jnp.cos(jnp.pi * (2.0 * place + 1.0) * freq / (2.0 * points)) * jnp.sqrt(2.0 / points)
    values = values.at[0].multiply(jnp.sqrt(0.5))
    rounded = lax.optimization_barrier(values.astype(jnp.bfloat16))
    return rounded.astype(jnp.float32)


def forward(square_low, cosines, cos_low):
    half = jnp.einsum("cab,jb->caj", square_low, cos_low, preferred_element_type=jnp.float32)
    return jnp.einsum("ia,caj->cij", cosines, half, precision=lax.Precision.HIGHEST)


def decode(dense_matrix, cosines):
    square = dense_matrix.reshape(dense_matrix.shape[0], BLOCK, BLOCK)
    half = jnp.einsum("cij,jb->cib", square, cosines, precision=lax.Precision.HIGHEST)
    full = jnp.einsum("ia,cib->cab", cosines, half, precision=lax.Precision.HIGHEST)
    return full.reshape(dense_matrix.shape[0], BLOCK * BLOCK)


def decode_sparse(dense_low, cosines, cos_low):
    square = dense_low.reshape(dense_low.shape[0], BLOCK, BLOCK)
    half = jnp.einsum("cij,jb->cib", square, cos_low, preferred_element_type=jnp.float32)
    full = jnp.einsum("ia,cib->cab", cosines, half, precision=lax.Precision.HIGHEST)
    return full.reshape(dense_low.shape[0], BLOCK * BLOCK)


def densify(values, spots):
    entries, columns = values.shape
    per_step = math.gcd(entries, max(1, 65536 // columns))
    positions = jnp.arange(BLOCK, dtype=jnp.int32)

    def one_block(pieces):
        block_values, block_spots = pieces
        zeros = jnp.zeros_like(block_values)
        row_onehot = jnp.where(
            (block_spots // BLOCK)[:, None, :] == positions[None, :, None],
            block_values[:, None, :],
            zeros[:, None, :],
        )
        column_onehot = ((block_spots % BLOCK)[:, None, :] == positions[None, :, None]).astype(
            jnp.bfloat16
        )
        dense_matrix = jnp.einsum(
            "bcy,bzy->bcz", row_onehot, column_onehot, preferred_element_type=jnp.float32
        )
        return dense_matrix.reshape(per_step, BLOCK * BLOCK)

    stacked = lax.map(
        one_block,
        (
            values.reshape(entries // per_step, per_step, columns),
            spots.reshape(entries // per_step, per_step, columns),
        ),
    )
    return stacked.reshape(entries, BLOCK * BLOCK)


def owner_sum(received):
    values, spots = received
    return densify(values[0], spots[0])


def local(momentum, picked, owner_span_order):
    cosines = dct_cosines(BLOCK)
    cos_low = cosines.astype(jnp.bfloat16)
    owners = lax.axis_size("grp")
    span_count = momentum.shape[0]
    square_low = momentum.reshape(span_count, BLOCK, BLOCK)
    transform_coefficients = forward(square_low, cosines, cos_low).reshape(
        span_count, BLOCK * BLOCK
    )
    chosen = jnp.take_along_axis(transform_coefficients, picked, axis=1).astype(jnp.bfloat16)
    own_dense = densify(chosen, picked).astype(jnp.bfloat16)
    residual_momentum = (
        momentum.astype(jnp.float32) - decode_sparse(own_dense, cosines, cos_low)
    ).astype(jnp.bfloat16)
    slot_values = jnp.take(chosen, owner_span_order, axis=0)
    slot_spots = jnp.take(picked, owner_span_order, axis=0)
    shaped = (slot_values.reshape(owners, CH_OWN, TOPK), slot_spots.reshape(owners, CH_OWN, TOPK))
    partial_sum = owner_sum(
        (
            lax.all_to_all(shaped[0], "grp", split_axis=0, concat_axis=2, tiled=True),
            lax.all_to_all(shaped[1], "grp", split_axis=0, concat_axis=2, tiled=True),
        )
    )
    partial_sum = lax.psum(partial_sum, "rep")
    my_share = decode(partial_sum, cosines).astype(jnp.bfloat16)
    update = lax.all_gather(my_share, "grp", axis=0, tiled=True)
    return (update, residual_momentum)


def solution(mesh):
    return jax.shard_map(
        local,
        mesh=mesh,
        in_specs=(P(("grp", "rep"), None), P(("grp", "rep"), None), P()),
        out_specs=(P(), P(("grp", "rep"), None)),
        check_vma=False,
    )
```

profile of v0, /device:TPU:0, one launch (start us, length us, event | category | flops | bytes accessed | tf_op | source)
XLA Modules:
  0.0 55.1 jit_solution(13529057157685993092)
XLA Ops:
  0.6 0.7 %compare_and_fusion = pred[8]{0:T(512)(128)(4,1)S(1)} fusion(s32[8]{0:T(128)} %param.7), kind=kLoop, calls=%fused_computation.49 | loop fusion | flops 48 | bytes 40 | tf_op jit(solution)/shard_map/jit(_take)/and | solution.py:90
  1.4 0.6 %copy-done = s32[8,32]{1,0:T(8,128)S(1)} copy-done((s32[8,32]{1,0:T(8,128)S(1)}, s32[8,32]{1,0:T(8,128)}, u32[]{:S(2)}) %copy-start) | copy-done | bytes 1048
  2.4 0.2 reshape.317
  2.5 0.3 convolution_bitcast_fusion.2
  2.8 0.3 convolution_bitcast_fusion.1
  3.2 0.2 reshape.318
  3.4 2.4 %gather_fusion.2 = bf16[256]{0:T(256)(128)(2,1)S(1)} fusion(bf16[8,4096]{1,0:T(8,128)(2,1)S(1)} %reshape.318, s32[256]{0:T(256)S(1)} %reshape.340), kind=kCustom, calls=%fused_computation.2 | custom fusion | bytes 3072 | tf_op jit(solution)/shard_map/jit(take_along_axis)/gather | solution.py:85
  5.9 0.6 %gather_fusion.1 = bf16[8,32]{1,0:T(8,128)(2,1)S(1)} fusion(bf16[8,32]{1,0:T(8,128)(2,1)S(1)} %select_convert_fusion, s32[1024]{0:T(1024)S(1)} %pad_clamp_fusion), kind=kCustom, calls=%fused_computation.1 | custom fusion | bytes 1056 | tf_op jit(solution)/shard_map/jit(_take)/gather | solution.py:90
  6.5 0.6 %copy.20 = bf16[8,1,32]{2,1,0:T(2,128)(2,1)} copy(bf16[8,1,32]{2,0,1:T(8,128)(2,1)S(1)} %bitcast_select_fusion.1) | data formatting | bytes 1024 | tf_op jit(solution)/shard_map/jit(_take)/select_n | solution.py:90
  7.1 5.2 %all-to-all-start.1 = ((bf16[8,1,32]{2,1,0:T(2,128)(2,1)}), bf16[8,1,32]{2,1,0:T(2,128)(2,1)S(1)}, u32[]{:S(2)}, u32[]{:S(2)}) async-start(bf16[8,1,32]{2,1,0:T(2,128)(2,1)} %copy.20), calls=%async_computation.1 | async-start | bytes 8192 | tf_op jit(solution)/shard_map/all_to_all | solution.py:95
  12.3 0.6 %gather_fusion = s32[8,32]{1,0:T(8,128)S(1)} fusion(s32[8,32]{1,0:T(8,128)S(1)} %copy-done, s32[1024]{0:T(1024)S(1)} %pad_clamp_fusion), kind=kCustom, calls=%fused_computation | custom fusion | bytes 2080 | tf_op jit(solution)/shard_map/jit(_take)/gather | solution.py:91
  12.9 0.6 %fusion = f32[8,64,64]{1,2,0:T(8,128)S(1)} fusion(s32[8,32]{1,0:T(8,128)S(1)} %get-tuple-element.45, s32[8,32]{1,0:T(8,128)S(1)} %get-tuple-element.44, bf16[8,32]{1,0:T(8,128)(2,1)S(1)} %select_convert_fusion, bf16[64,64]{1,0:T(8,128)(2,1)S(1)} %convert_element_type.42), kind=kOutput, calls=%fused_computation.7 | convolution fusion | flops 6373376 | bytes 141824 | tf_op jit(solution)/shard_map/cij,jb->cib/dot_general | solution.py:35
  13.5 0.3 convolution_bitcast_fusion
  13.8 0.7 %bitcast_select_fusion = s32[8,1,32]{2,0,1:T(8,128)} fusion(s32[8,32]{1,0:T(8,128)S(1)} %gather_fusion, pred[8]{0:T(512)(128)(4,1)S(1)} %compare_and_fusion), kind=kLoop, calls=%fused_computation.40 | loop fusion | flops 256 | bytes 2056 | tf_op jit(solution)/shard_map/jit(_take)/select_n | solution.py:91
  14.7 2.3 %all-to-all-done.1 = bf16[8,1,32]{2,1,0:T(2,128)(2,1)S(1)} async-done(((bf16[8,1,32]{2,1,0:T(2,128)(2,1)}), bf16[8,1,32]{2,1,0:T(2,128)(2,1)S(1)}, u32[]{:S(2)}, u32[]{:S(2)}) %all-to-all-start.1) | async-done | bytes 544 | tf_op jit(solution)/shard_map/all_to_all | solution.py:95
  16.9 3.3 %all-to-all-start = ((s32[8,1,32]{2,1,0:T(1,128)}), s32[8,1,32]{2,1,0:T(1,128)S(1)}, u32[]{:S(2)}, u32[]{:S(2)}) async-start(s32[8,1,32]{2,1,0:T(1,128)} %bitcast.1), calls=%async_computation | async-start | bytes 8192 | tf_op jit(solution)/shard_map/all_to_all | solution.py:96
  20.3 0.6 %subtract_convert_fusion = bf16[8,4096]{1,0:T(8,128)(2,1)} fusion(f32[8,4096]{1,0:T(8,128)S(1)} %reshape.322, bf16[8,4096]{1,0:T(8,128)(2,1)S(1)} %copy-done.1), kind=kLoop, calls=%fused_computation.10 | loop fusion | flops 98304 | bytes 262144 | tf_op jit(solution)/shard_map/convert_element_type | solution.py:89
  21.0 3.8 %all-to-all-done = s32[8,1,32]{2,1,0:T(1,128)S(1)} async-done(((s32[8,1,32]{2,1,0:T(1,128)}), s32[8,1,32]{2,1,0:T(1,128)S(1)}, u32[]{:S(2)}, u32[]{:S(2)}) %all-to-all-start) | async-done | bytes 1056 | tf_op jit(solution)/shard_map/all_to_all | solution.py:96
  24.8 0.5 broadcast.298
  25.3 0.7 %reduce.6 = s32[8,32]{1,0:T(8,128)S(1)} reduce(s32[8,1,32]{2,1,0:T(1,128)S(1)} %all-to-all-done, s32[]{:T(128)} %broadcast.298), dimensions={1}, to_apply=%all_to_all.4.reduce_sub_computation.3 | reduce | bytes 2052 | tf_op jit(solution)/shard_map/all_to_all | solution.py:96
  26.2 19.4 %psum.7 = f32[64,64]{1,0:T(8,128)S(1)} all-reduce(f32[64,64]{1,0:T(8,128)S(1)} %fusion.10), channel_id=1, replica_groups=mesh['grp'=8,'rep'=4] {'rep'}, use_global_device_ids=true, to_apply=%region_0.0 | all-reduce | flops 4096 | bytes 32768 | tf_op jit(solution)/shard_map/psum | solution.py:99
  45.7 0.2 fusion.1
  46.2 8.3 %all-gather = bf16[8,1,4096]{2,1,0:T(2,128)(2,1)S(1)} all-gather(bf16[1,1,4096]{2,1,0:T(2,128)(2,1)S(1)} %reshape.353), channel_id=1, replica_groups=mesh['grp'=8,'rep'=4] {'grp'}, dimensions={0}, use_global_device_ids=true | all-gather | bytes 73728 | tf_op jit(solution)/shard_map/all_gather | solution.py:101
  54.4 0.7 %copy.27 = bf16[8,1,4096]{2,0,1:T(8,128)(2,1)} copy(bf16[8,1,4096]{2,1,0:T(2,128)(2,1)S(1)} %all-gather) | data formatting | bytes 131072
  (29 shorter events, 1.5 us)
Async XLA Ops:
  0.6 0.7 %copy-start.2 = (s32[8]{0:T(128)S(1)}, s32[8]{0:T(128)}, u32[]{:S(2)}) copy-start(s32[8]{0:T(128)} %param.7) | copy-start | bytes 100
  1.4 0.7 %copy-start = (s32[8,32]{1,0:T(8,128)S(1)}, s32[8,32]{1,0:T(8,128)}, u32[]{:S(2)}) copy-start(s32[8,32]{1,0:T(8,128)} %param.6) | copy-start | bytes 3076
  1.4 1.0 %copy-start.1 = (bf16[8,4096]{1,0:T(8,128)(2,1)S(1)}, bf16[8,4096]{1,0:T(8,128)(2,1)}, u32[]{:S(2)}) copy-start(bf16[8,4096]{1,0:T(8,128)(2,1)} %param.5) | copy-start | bytes 196612
  7.1 9.8 %all-to-all-start.1 = ((bf16[8,1,32]{2,1,0:T(2,128)(2,1)}), bf16[8,1,32]{2,1,0:T(2,128)(2,1)S(1)}, u32[]{:S(2)}, u32[]{:S(2)}) async-start(bf16[8,1,32]{2,1,0:T(2,128)(2,1)} %copy.20), calls=%async_computation.1 | async-start | bytes 8192 | tf_op jit(solution)/shard_map/all_to_all | solution.py:95
  16.9 7.9 %all-to-all-start = ((s32[8,1,32]{2,1,0:T(1,128)}), s32[8,1,32]{2,1,0:T(1,128)S(1)}, u32[]{:S(2)}, u32[]{:S(2)}) async-start(s32[8,1,32]{2,1,0:T(1,128)} %bitcast.1), calls=%async_computation | async-start | bytes 8192 | tf_op jit(solution)/shard_map/all_to_all | solution.py:96
where the time goes:
time: 55.4 us; the launch traced here: 55.1 us
  blocking collectives  27.6 us (50%)
  starting transfers between devices  8.52 us (15%)
  local copies, waits for them, and re-layouts  7.25 us (13%)
  waiting for transfers between devices  6.04 us (11%)
  other arithmetic  3 us (5%)
  matrix products  1.86 us (3%)
  between operations  0.8 us (1%)
    psum x1, blocking collectives, local(): partial_sum = lax.psum(partial_sum, 'rep')  19.4 us
    all_gather x1, blocking collectives, local(): update = lax.all_gather(my_share, 'grp', axis=0, tiled=True)  8.26 us
    all_to_all x1, starting transfers between devices, local(): lax.all_to_all(shaped[0], 'grp', split_axis=0, concat_axis=2, tiled=True)  5.21 us
    all_to_all x1, waiting for transfers between devices, local(): lax.all_to_all(shaped[1], 'grp', split_axis=0, concat_axis=2, tiled=True)  3.79 us
    all_to_all x1, starting transfers between devices, local(): lax.all_to_all(shaped[1], 'grp', split_axis=0, concat_axis=2, tiled=True)  3.31 us
    gather x3, local copies, waits for them, and re-layouts, local(): jnp.take_along_axis(transform_coefficients, picked, axis=1)  2.56 us
    all_to_all x1, waiting for transfers between devices, local(): lax.all_to_all(shaped[0], 'grp', split_axis=0, concat_axis=2, tiled=True)  2.26 us
    unnamed x8, local copies, waits for them, and re-layouts  1.44 us
  transfers between devices with their start and end apart: 2, of which 2 were waited for; matrix products, arithmetic and copies ran while one was open for 6% of the time, Pallas kernels for 0%

commit v1 on v0

--- a/solution.py
+++ b/solution.py
@@ -92,7 +92,12 @@
     shaped = (slot_values.reshape(owners, CH_OWN, TOPK), slot_spots.reshape(owners, CH_OWN, TOPK))
     partial_sum = owner_sum(
         (
-            lax.all_to_all(shaped[0], "grp", split_axis=0, concat_axis=2, tiled=True),
+            jnp.concatenate(
+                lax.all_to_all(
+                    jnp.stack(jnp.split(shaped[0], lax.axis_size("grp"), axis=0)), "grp", 0, 0
+                ),
+                axis=2,
+            ),
             lax.all_to_all(shaped[1], "grp", split_axis=0, concat_axis=2, tiled=True),
         )
     )

time: 55.4 us -> 59 us (1.065)
  local copies, waits for them, and re-layouts: 7.25 us -> 10.8 us
    unnamed x8 -> x15, local copies, waits for them, and re-layouts: 1.44 us -> 5.04 us
    select_n x1 -> x0, local copies, waits for them, and re-layouts: 0.6 us -> none  [local(): slot_values = jnp.take(chosen, owner_span_order, axis=0)]
  transfers between devices with their start and end apart: 2 -> 2, of which waited for: 2 -> 2; matrix products, arithmetic and copies ran while one was open for 6% -> 5% of each run, Pallas kernels for 0% -> 0%
where the time goes in v1:
time: 59 us; the launch traced here: 58.6 us
  blocking collectives  27.6 us (47%)
  local copies, waits for them, and re-layouts  10.8 us (18%)
  starting transfers between devices  8.52 us (14%)
  waiting for transfers between devices  6.04 us (10%)
  other arithmetic  3 us (5%)
  matrix products  1.86 us (3%)
  between operations  0.8 us (1%)
    psum x1, blocking collectives, local(): partial_sum = lax.psum(partial_sum, 'rep')  19.4 us
    all_gather x1, blocking collectives, local(): update = lax.all_gather(my_share, 'grp', axis=0, tiled=True)  8.26 us
    all_to_all x1, starting transfers between devices, local(): lax.all_to_all(jnp.stack(jnp.split(shaped[0], lax.axis_size('grp'), axis=...  5.21 us
    unnamed x15, local copies, waits for them, and re-layouts  5.04 us
    all_to_all x1, waiting for transfers between devices, local(): lax.all_to_all(shaped[1], 'grp', split_axis=0, concat_axis=2, tiled=True)  3.79 us
    all_to_all x1, starting transfers between devices, local(): lax.all_to_all(shaped[1], 'grp', split_axis=0, concat_axis=2, tiled=True)  3.31 us
    gather x3, local copies, waits for them, and re-layouts, local(): jnp.take_along_axis(transform_coefficients, picked, axis=1)  2.56 us
    all_to_all x1, waiting for transfers between devices, local(): lax.all_to_all(jnp.stack(jnp.split(shaped[0], lax.axis_size('grp'), axis=...  2.26 us
  transfers between devices with their start and end apart: 2, of which 2 were waited for; matrix products, arithmetic and copies ran while one was open for 5% of the time, Pallas kernels for 0%

profile of v1, /device:TPU:0, one launch (start us, length us, event | category | flops | bytes accessed | tf_op | source)
XLA Modules:
  0.0 58.6 jit_solution(15837122790695342909)
XLA Ops:
  0.6 0.7 %compare_and_fusion = pred[8]{0:T(512)(128)(4,1)S(1)} fusion(s32[8]{0:T(128)} %param.7), kind=kLoop, calls=%fused_computation.57 | loop fusion | flops 48 | bytes 40 | tf_op jit(solution)/shard_map/jit(_take)/and | solution.py:90
  1.4 0.6 %copy-done = s32[8,32]{1,0:T(8,128)S(1)} copy-done((s32[8,32]{1,0:T(8,128)S(1)}, s32[8,32]{1,0:T(8,128)}, u32[]{:S(2)}) %copy-start) | copy-done | bytes 1048
  3.4 2.4 %gather_fusion.2 = bf16[256]{0:T(256)(128)(2,1)S(1)} fusion(bf16[8,4096]{1,0:T(8,128)(2,1)S(1)} %reshape.308, s32[256]{0:T(256)S(1)} %reshape.330), kind=kCustom, calls=%fused_computation.2 | custom fusion | bytes 3072 | tf_op jit(solution)/shard_map/jit(take_along_axis)/gather | solution.py:85
  5.9 0.6 gather_fusion.1
  6.5 0.5 constant_dynamic-update-slice_fusion.7
  7.0 0.5 constant_dynamic-update-slice_fusion.6
  7.5 0.5 constant_dynamic-update-slice_fusion.5
  8.1 0.5 constant_dynamic-update-slice_fusion.4
  8.6 0.5 constant_dynamic-update-slice_fusion.3
  9.1 0.5 constant_dynamic-update-slice_fusion.2
  9.6 0.5 constant_dynamic-update-slice_fusion.1
  10.1 0.5 constant_dynamic-update-slice_fusion
  10.6 5.2 %all-to-all-start.1 = ((bf16[8,1,1,32]{3,2,1,0:T(2,128)(2,1)}), bf16[8,1,1,32]{3,2,1,0:T(2,128)(2,1)S(1)}, u32[]{:S(2)}, u32[]{:S(2)}) async-start(bf16[8,1,1,32]{3,2,1,0:T(2,128)(2,1)} %constant_dynamic-update-slice_fusion), calls=%async_computation.1 | async-start | bytes 8192 | tf_op jit(solution)/shard_map/all_to_all | solution.py:96
  15.8 0.6 gather_fusion
  16.4 0.6 %fusion = f32[8,64,64]{1,2,0:T(8,128)S(1)} fusion(s32[8,32]{1,0:T(8,128)S(1)} %get-tuple-element.45, s32[8,32]{1,0:T(8,128)S(1)} %get-tuple-element.44, bf16[8,32]{1,0:T(8,128)(2,1)S(1)} %select_convert_fusion, bf16[64,64]{1,0:T(8,128)(2,1)S(1)} %convert_element_type.42), kind=kOutput, calls=%fused_computation.7 | convolution fusion | flops 6373376 | bytes 141824 | tf_op jit(solution)/shard_map/cij,jb->cib/dot_general | solution.py:35
  17.3 0.7 %bitcast_select_fusion = s32[8,1,32]{2,0,1:T(8,128)} fusion(s32[8,32]{1,0:T(8,128)S(1)} %gather_fusion, pred[8]{0:T(512)(128)(4,1)S(1)} %compare_and_fusion), kind=kLoop, calls=%fused_computation.48 | loop fusion | flops 256 | bytes 2056 | tf_op jit(solution)/shard_map/jit(_take)/select_n | solution.py:91
  18.2 2.3 %all-to-all-done.1 = bf16[8,1,1,32]{3,2,1,0:T(2,128)(2,1)S(1)} async-done(((bf16[8,1,1,32]{3,2,1,0:T(2,128)(2,1)}), bf16[8,1,1,32]{3,2,1,0:T(2,128)(2,1)S(1)}, u32[]{:S(2)}, u32[]{:S(2)}) %all-to-all-start.1) | async-done | bytes 544 | tf_op jit(solution)/shard_map/all_to_all | solution.py:96
  20.5 3.3 %all-to-all-start = ((s32[8,1,32]{2,1,0:T(1,128)}), s32[8,1,32]{2,1,0:T(1,128)S(1)}, u32[]{:S(2)}, u32[]{:S(2)}) async-start(s32[8,1,32]{2,1,0:T(1,128)} %bitcast.1), calls=%async_computation | async-start | bytes 8192 | tf_op jit(solution)/shard_map/all_to_all | solution.py:101
  23.8 0.6 %subtract_convert_fusion = bf16[8,4096]{1,0:T(8,128)(2,1)} fusion(f32[8,4096]{1,0:T(8,128)S(1)} %reshape.312, bf16[8,4096]{1,0:T(8,128)(2,1)S(1)} %copy-done.1), kind=kLoop, calls=%fused_computation.10 | loop fusion | flops 98304 | bytes 262144 | tf_op jit(solution)/shard_map/convert_element_type | solution.py:89
  24.5 3.8 %all-to-all-done = s32[8,1,32]{2,1,0:T(1,128)S(1)} async-done(((s32[8,1,32]{2,1,0:T(1,128)}), s32[8,1,32]{2,1,0:T(1,128)S(1)}, u32[]{:S(2)}, u32[]{:S(2)}) %all-to-all-start) | async-done | bytes 1056 | tf_op jit(solution)/shard_map/all_to_all | solution.py:101
  28.8 0.7 %reduce.6 = s32[8,32]{1,0:T(8,128)S(1)} reduce(s32[8,1,32]{2,1,0:T(1,128)S(1)} %all-to-all-done, s32[]{:T(128)} %broadcast.276), dimensions={1}, to_apply=%all_to_all.4.reduce_sub_computation.3 | reduce | bytes 2052 | tf_op jit(solution)/shard_map/all_to_all | solution.py:101
  29.7 19.4 %psum.7 = f32[64,64]{1,0:T(8,128)S(1)} all-reduce(f32[64,64]{1,0:T(8,128)S(1)} %fusion.10), channel_id=1, replica_groups=mesh['grp'=8,'rep'=4] {'rep'}, use_global_device_ids=true, to_apply=%region_0.0 | all-reduce | flops 4096 | bytes 32768 | tf_op jit(solution)/shard_map/psum | solution.py:104
  49.7 8.3 %all-gather = bf16[8,1,4096]{2,1,0:T(2,128)(2,1)S(1)} all-gather(bf16[1,1,4096]{2,1,0:T(2,128)(2,1)S(1)} %reshape.343), channel_id=1, replica_groups=mesh['grp'=8,'rep'=4] {'grp'}, dimensions={0}, use_global_device_ids=true | all-gather | bytes 73728 | tf_op jit(solution)/shard_map/all_gather | solution.py:106
  57.9 0.7 %copy.20 = bf16[8,1,4096]{2,0,1:T(8,128)(2,1)} copy(bf16[8,1,4096]{2,1,0:T(2,128)(2,1)S(1)} %all-gather) | data formatting | bytes 131072
  (36 shorter events, 3.4 us)
Async XLA Ops:
  0.6 0.7 %copy-start.2 = (s32[8]{0:T(128)S(1)}, s32[8]{0:T(128)}, u32[]{:S(2)}) copy-start(s32[8]{0:T(128)} %param.7) | copy-start | bytes 100
  1.4 0.7 %copy-start = (s32[8,32]{1,0:T(8,128)S(1)}, s32[8,32]{1,0:T(8,128)}, u32[]{:S(2)}) copy-start(s32[8,32]{1,0:T(8,128)} %param.6) | copy-start | bytes 3076
  1.4 1.0 %copy-start.1 = (bf16[8,4096]{1,0:T(8,128)(2,1)S(1)}, bf16[8,4096]{1,0:T(8,128)(2,1)}, u32[]{:S(2)}) copy-start(bf16[8,4096]{1,0:T(8,128)(2,1)} %param.5) | copy-start | bytes 196612
  10.6 9.8 %all-to-all-start.1 = ((bf16[8,1,1,32]{3,2,1,0:T(2,128)(2,1)}), bf16[8,1,1,32]{3,2,1,0:T(2,128)(2,1)S(1)}, u32[]{:S(2)}, u32[]{:S(2)}) async-start(bf16[8,1,1,32]{3,2,1,0:T(2,128)(2,1)} %constant_dynamic-update-slice_fusion), calls=%async_computation.1 | async-start | bytes 8192 | tf_op jit(solution)/shard_map/all_to_all | solution.py:96
  20.5 7.9 %all-to-all-start = ((s32[8,1,32]{2,1,0:T(1,128)}), s32[8,1,32]{2,1,0:T(1,128)S(1)}, u32[]{:S(2)}, u32[]{:S(2)}) async-start(s32[8,1,32]{2,1,0:T(1,128)} %bitcast.1), calls=%async_computation | async-start | bytes 8192 | tf_op jit(solution)/shard_map/all_to_all | solution.py:101
